TPU v7x, 32 devices: a whole 2x2x4 slice. The times are simulated.
32 devices in a mesh: row: 16 (over z, y, core), col: 2 (over x).
Axes of the slice: x: 2, y: 2, z: 4, core: 2. Of those that a mesh axis runs over, the one named last changes fastest.
Arguments:
- pair_act: bfloat16 [192, 192, 128], P('row', 'col'), may hold values from -6 to 6
- tile_mask: int32 [12, 12], replicated, may hold values 0 or 1
- w_left_gate: bfloat16 [128, 128], replicated, may hold values from -0.5 to 0.5
- w_left: bfloat16 [128, 128], replicated, may hold values from -0.5 to 0.5
- w_right_gate: bfloat16 [128, 128], replicated, may hold values from -0.5 to 0.5
- w_right: bfloat16 [128, 128], replicated, may hold values from -0.5 to 0.5
- w_out_gate: bfloat16 [128, 128], replicated, may hold values from -0.5 to 0.5
- w_out: bfloat16 [128, 128], replicated, may hold values from -0.5 to 0.5
Outputs:
- update: bfloat16 [192, 192, 128], P('row', 'col')
All inputs are finite; a program needn't handle non-finite values.
Results may differ from a plain program's by a relative error of at most 0.0083.
Values may be sent and summed in bfloat16 or wider, within the bound.
A program may use at most 64 MiB of HBM per device.

v0:
```python
import jax
import jax.numpy as jnp
from jax import lax
from jax.sharding import PartitionSpec as P

TILES = 12


def norm_axis(values, axis):
    mean = jnp.mean(values, axis=axis, keepdims=True)
    centred = values - mean
    spread = jnp.mean(centred * centred, axis=axis, keepdims=True)
    return centred * lax.rsqrt(spread + 1e-05)


def local(pair_act, tile_mask, w_left_gate, w_left, w_right_gate, w_right, w_out_gate, w_out):
    rows, cols, width = pair_act.shape
    residues = rows * lax.axis_size("row")
    tile = residues // TILES
    normed = norm_axis(pair_act.astype(jnp.float32), 2).astype(jnp.bfloat16)
    tile_range = lax.iota(jnp.int32, TILES)
    row_ids = (lax.axis_index("row") * rows + lax.iota(jnp.int32, rows)) // tile
    col_ids = (lax.axis_index("col") * cols + lax.iota(jnp.int32, cols)) // tile
    row_hot = (row_ids[:, None] == tile_range[None, :]).astype(jnp.float32)
    col_hot = (col_ids[:, None] == tile_range[None, :]).astype(jnp.float32)
    pair_mask = jnp.dot(
        jnp.dot(row_hot, tile_mask.astype(jnp.float32), preferred_element_type=jnp.float32),
        col_hot.T,
        preferred_element_type=jnp.float32,
    )

    def project(weight):
        return jnp.einsum("ijd,de->eij", normed, weight, preferred_element_type=jnp.float32)

    left = (jax.nn.sigmoid(project(w_left_gate)) * project(w_left) * pair_mask[None]).astype(
        jnp.bfloat16
    )
    right = (jax.nn.sigmoid(project(w_right_gate)) * project(w_right) * pair_mask[None]).astype(
        jnp.bfloat16
    )
    left_rows, right_rows = (
        lax.all_to_all(left, "row", split_axis=0, concat_axis=1, tiled=True),
        lax.all_to_all(right, "row", split_axis=0, concat_axis=1, tiled=True),
    )
    right_block = lax.all_to_all(right_rows, "col", split_axis=1, concat_axis=2, tiled=True)
    triangle = jnp.einsum(
        "cik,cjk->jci",
        lax.all_gather(left_rows, "col", axis=2, tiled=True),
        right_block,
        preferred_element_type=jnp.float32,
    )
    triangle = triangle.astype(jnp.bfloat16)
    owned = lax.all_to_all(triangle, "row", split_axis=2, concat_axis=1, tiled=True)
    scaled = norm_axis(owned.astype(jnp.float32), 1).astype(jnp.bfloat16)
    projected = jnp.einsum("jci,ce->ije", scaled, w_out, preferred_element_type=jnp.float32)
    gate = jax.nn.sigmoid(
        jnp.einsum("ijd,de->ije", normed, w_out_gate, preferred_element_type=jnp.float32)
    )
    return (gate * projected).astype(jnp.bfloat16)


def solution(mesh):
    return jax.shard_map(
        local,
        mesh=mesh,
        in_specs=(P("row", "col", None), P(), P(), P(), P(), P(), P(), P()),
        out_specs=P("row", "col", None),
        check_vma=False,
    )
```

profile of v0, /device:TPU:0, one launch (start us, length us, event | category | flops | bytes accessed | tf_op | source)
XLA Modules:
  0.0 84.8 jit_solution(9804419726071187752)
XLA Ops:
  0.0 0.0 copy-start
  0.0 0.0 copy-start.1
  0.0 1.2 %convert_reduce_fusion = f32[12,96]{1,0:T(8,128)S(1)} fusion(bf16[12,96,128]{2,1,0:T(8,128)(2,1)} %param.8), kind=kLoop, calls=%fused_computation.34 | loop fusion | flops 293760 | bytes 299520 | tf_op jit(solution)/shard_map/reduce_sum | solution.py:10
  1.2 0.0 copy-done.1
  1.2 0.5 fusion.26
  1.7 0.0 copy-done
  1.7 0.0 copy-start.7
  1.7 0.8 fusion.8
  2.5 0.0 copy-done.7
  2.5 0.0 copy-start.2
  2.5 0.3 fusion.18
  2.8 0.5 copy-done.2
  3.3 0.5 fusion.17
  3.8 1.2 %copy.22 = bf16[128,12,96]{2,1,0:T(8,128)(2,1)} copy(bf16[128,12,96]{0,2,1:T(8,128)(2,1)S(1)} %fusion.17) | data formatting | bytes 589824 | tf_op jit(solution)/shard_map/convert_element_type | solution.py:38
  5.0 0.0 copy-start.5
  5.0 7.5 %all-to-all-start = ((bf16[128,12,96]{2,1,0:T(8,128)(2,1)}), bf16[128,12,96]{2,1,0:T(8,128)(2,1)S(1)}, u32[]{:S(2)}, u32[]{:S(2)}) async-start(bf16[128,12,96]{2,1,0:T(8,128)(2,1)} %copy.22), calls=%async_computation | async-start | bytes 1048576 | tf_op jit(solution)/shard_map/all_to_all | solution.py:43
  12.6 0.0 copy-done.5
  12.6 0.0 copy-start.3
  12.6 0.8 fusion.5
  13.4 0.0 copy-done.3
  13.4 0.5 fusion.16
  13.9 1.2 %copy.27 = bf16[128,12,96]{2,1,0:T(8,128)(2,1)} copy(bf16[128,12,96]{0,2,1:T(8,128)(2,1)S(1)} %fusion.16) | data formatting | bytes 589824 | tf_op jit(solution)/shard_map/convert_element_type | solution.py:35
  15.1 11.7 %all-to-all-done = bf16[128,12,96]{2,1,0:T(8,128)(2,1)S(1)} async-done(((bf16[128,12,96]{2,1,0:T(8,128)(2,1)}), bf16[128,12,96]{2,1,0:T(8,128)(2,1)S(1)}, u32[]{:S(2)}, u32[]{:S(2)}) %all-to-all-start) | async-done | bytes 294944 | tf_op jit(solution)/shard_map/all_to_all | solution.py:43
  26.8 4.2 %all-to-all-start.2 = ((bf16[128,12,96]{2,1,0:T(8,128)(2,1)}), bf16[128,12,96]{2,1,0:T(8,128)(2,1)S(1)}, u32[]{:S(2)}, u32[]{:S(2)}) async-start(bf16[128,12,96]{2,1,0:T(8,128)(2,1)} %copy.27), calls=%async_computation.2 | async-start | bytes 1048576 | tf_op jit(solution)/shard_map/all_to_all | solution.py:42
  31.0 0.8 copy.24
  31.9 13.4 %all-to-all-done.2 = bf16[128,12,96]{2,1,0:T(8,128)(2,1)S(1)} async-done(((bf16[128,12,96]{2,1,0:T(8,128)(2,1)}), bf16[128,12,96]{2,1,0:T(8,128)(2,1)S(1)}, u32[]{:S(2)}, u32[]{:S(2)}) %all-to-all-start.2) | async-done | bytes 294944 | tf_op jit(solution)/shard_map/all_to_all | solution.py:42
  45.3 3.5 %all-to-all-start.1 = ((bf16[8,192,96]{2,0,1:T(8,128)(2,1)}), bf16[8,192,96]{2,0,1:T(8,128)(2,1)S(1)}, u32[]{:S(2)}, u32[]{:S(2)}) async-start(bf16[8,192,96]{2,0,1:T(8,128)(2,1)} %bitcast.7), calls=%async_computation.1 | async-start | bytes 786432 | tf_op jit(solution)/shard_map/all_to_all | solution.py:45
  48.8 0.1 copy.29
  48.9 0.4 copy.30
  49.3 15.0 %all_gather.3 = bf16[8,192,192]{1,0,2:T(8,128)(2,1)S(1)} all-gather(bf16[8,192,96]{1,0,2:T(8,128)(2,1)S(1)} %copy.30), channel_id=1, replica_groups=mesh['row'=16,'col'=2] {'col'}, dimensions={2}, use_global_device_ids=true | all-gather | bytes 884736 | tf_op jit(solution)/shard_map/all_gather | solution.py:48
  64.3 0.0 all-to-all-done.1
  64.3 0.4 copy.26
  64.7 0.2 all_to_all.53
  65.0 0.3 fusion.15
  65.3 1.0 %copy.32 = bf16[96,8,192]{0,1,2:T(8,128)(2,1)} copy(bf16[96,8,192]{2,0,1:T(8,128)(2,1)S(1)} %fusion.15) | data formatting | bytes 589824 | tf_op jit(solution)/shard_map/convert_element_type | solution.py:52
  66.2 0.0 copy-start.6
  66.2 4.5 %all-to-all-start.3 = ((bf16[96,8,192]{0,1,2:T(8,128)(2,1)}), bf16[96,8,192]{0,1,2:T(8,128)(2,1)S(1)}, u32[]{:S(2)}, u32[]{:S(2)}) async-start(bf16[96,8,192]{0,1,2:T(8,128)(2,1)} %copy.32), calls=%async_computation.3 | async-start | bytes 786432 | tf_op jit(solution)/shard_map/all_to_all | solution.py:53
  70.8 0.0 copy-done.6
  70.8 0.8 fusion.11
  71.6 11.4 %all-to-all-done.3 = bf16[96,8,192]{0,1,2:T(8,128)(2,1)S(1)} async-done(((bf16[96,8,192]{0,1,2:T(8,128)(2,1)}), bf16[96,8,192]{0,1,2:T(8,128)(2,1)S(1)}, u32[]{:S(2)}, u32[]{:S(2)}) %all-to-all-start.3) | async-done | bytes 294944 | tf_op jit(solution)/shard_map/all_to_all | solution.py:53
  83.0 0.1 fusion.29
  83.1 0.0 copy-start.4
  83.1 0.1 multiply_reduce_fusion
  83.2 0.6 copy-done.4
  83.8 1.0 %fusion.14 = bf16[12,96,128]{2,1,0:T(8,128)(2,1)} fusion(f32[12,96,128]{2,1,0:T(8,128)S(1)} %fusion.11, f32[96,12]{0,1:T(8,128)S(1)} %add_rsqrt_fusion, f32[96,12]{0,1:T(8,128)S(1)} %broadcast_multiply_fusion, bf16[128,128]{1,0:T(8,128)(2,1)S(1)} %copy-done.4, bf16[96,8,16,12]{0,1,3,2:T(8,128)(2,1)S(1)} %bitcast.61), kind=kOutput, calls=%fused_computation.21 | convolution fusion | flops 38633472 | bytes 1221632 | tf_op jit(solution)/shard_map/jci,ce->ije/dot_general | solution.py:55
  (6 shorter events, 0.0 us)
Async XLA Ops:
  0.0 1.7 %copy-start = (bf16[128,128]{1,0:T(8,128)(2,1)S(1)}, bf16[128,128]{1,0:T(8,128)(2,1)}, u32[]{:S(2)}) copy-start(bf16[128,128]{1,0:T(8,128)(2,1)} %param.12) | copy-start | bytes 98308
  0.0 1.2 %copy-start.1 = (bf16[12,96,128]{2,1,0:T(8,128)(2,1)S(1)}, bf16[12,96,128]{2,1,0:T(8,128)(2,1)}, u32[]{:S(2)}) copy-start(bf16[12,96,128]{2,1,0:T(8,128)(2,1)} %param.8) | copy-start | bytes 884740
  1.7 0.8 copy-start.7
  2.5 0.8 copy-start.2
  5.0 7.6 %copy-start.5 = (bf16[128,128]{1,0:T(8,128)(2,1)S(1)}, bf16[128,128]{1,0:T(8,128)(2,1)}, u32[]{:S(2)}) copy-start(bf16[128,128]{1,0:T(8,128)(2,1)} %param.10) | copy-start | bytes 98308
  5.0 21.8 %all-to-all-start = ((bf16[128,12,96]{2,1,0:T(8,128)(2,1)}), bf16[128,12,96]{2,1,0:T(8,128)(2,1)S(1)}, u32[]{:S(2)}, u32[]{:S(2)}) async-start(bf16[128,12,96]{2,1,0:T(8,128)(2,1)} %copy.22), calls=%async_computation | async-start | bytes 1048576 | tf_op jit(solution)/shard_map/all_to_all | solution.py:43
  12.6 0.8 copy-start.3
  26.8 18.4 %all-to-all-start.2 = ((bf16[128,12,96]{2,1,0:T(8,128)(2,1)}), bf16[128,12,96]{2,1,0:T(8,128)(2,1)S(1)}, u32[]{:S(2)}, u32[]{:S(2)}) async-start(bf16[128,12,96]{2,1,0:T(8,128)(2,1)} %copy.27), calls=%async_computation.2 | async-start | bytes 1048576 | tf_op jit(solution)/shard_map/all_to_all | solution.py:42
  45.3 19.0 %all-to-all-start.1 = ((bf16[8,192,96]{2,0,1:T(8,128)(2,1)}), bf16[8,192,96]{2,0,1:T(8,128)(2,1)S(1)}, u32[]{:S(2)}, u32[]{:S(2)}) async-start(bf16[8,192,96]{2,0,1:T(8,128)(2,1)} %bitcast.7), calls=%async_computation.1 | async-start | bytes 786432 | tf_op jit(solution)/shard_map/all_to_all | solution.py:45
  66.2 4.6 %copy-start.6 = (bf16[128,128]{1,0:T(8,128)(2,1)S(1)}, bf16[128,128]{1,0:T(8,128)(2,1)}, u32[]{:S(2)}) copy-start(bf16[128,128]{1,0:T(8,128)(2,1)} %param.14) | copy-start | bytes 98308
  66.2 16.7 %all-to-all-start.3 = ((bf16[96,8,192]{0,1,2:T(8,128)(2,1)}), bf16[96,8,192]{0,1,2:T(8,128)(2,1)S(1)}, u32[]{:S(2)}, u32[]{:S(2)}) async-start(bf16[96,8,192]{0,1,2:T(8,128)(2,1)} %copy.32), calls=%async_computation.3 | async-start | bytes 786432 | tf_op jit(solution)/shard_map/all_to_all | solution.py:53
  83.1 0.8 copy-start.4
where the time goes:
time: 85.6 us; the launch traced here: 84.8 us
  waiting for transfers between devices  36.5 us (43%)
  starting transfers between devices  19.7 us (23%)
  blocking collectives  15 us (18%)
  local copies, waits for them, and re-layouts  6.45 us (8%)
  matrix products  4.94 us (6%)
  other arithmetic  1.92 us (2%)
    all_gather x1, blocking collectives, local(): lax.all_gather(left_rows, 'col', axis=2, tiled=True)  15 us
    all_to_all x1, waiting for transfers between devices, local(): lax.all_to_all(left, 'row', split_axis=0, concat_axis=1, tiled=True)  13.4 us
    all_to_all x1, waiting for transfers between devices, local(): lax.all_to_all(right, 'row', split_axis=0, concat_axis=1, tiled=True)  11.7 us
    all_to_all x1, waiting for transfers between devices, local(): lax.all_to_all(triangle, 'row', split_axis=2, concat_axis=1, tiled=True)  11.4 us
    all_to_all x1, starting transfers between devices, local(): lax.all_to_all(right, 'row', split_axis=0, concat_axis=1, tiled=True)  7.55 us
    all_to_all x1, starting transfers between devices, local(): lax.all_to_all(triangle, 'row', split_axis=2, concat_axis=1, tiled=True)  4.54 us
    all_to_all x1, starting transfers between devices, local(): lax.all_to_all(left, 'row', split_axis=0, concat_axis=1, tiled=True)  4.16 us
    all_to_all x1, starting transfers between devices, local(): lax.all_to_all(right_rows, 'col', split_axis=1, concat_axis=2, tiled=True)  3.47 us
  transfers between devices with their start and end apart: 4, of which 3 were waited for; matrix products, arithmetic and copies ran while one was open for 5% of the time, Pallas kernels for 0%

commit v1 on v0

--- a/solution.py
+++ b/solution.py
@@ -40,7 +40,10 @@
     )
     left_rows, right_rows = (
         lax.all_to_all(left, "row", split_axis=0, concat_axis=1, tiled=True),
-        lax.all_to_all(right, "row", split_axis=0, concat_axis=1, tiled=True),
+        jnp.concatenate(
+            lax.all_to_all(jnp.stack(jnp.split(right, lax.axis_size("row"), axis=0)), "row", 0, 0),
+            axis=1,
+        ),
     )
     right_block = lax.all_to_all(right_rows, "col", split_axis=1, concat_axis=2, tiled=True)
     triangle = jnp.einsum(

time: 85.6 us -> 102 us (1.19)
  blocking collectives: 15 us -> 32.5 us
  local copies, waits for them, and re-layouts: 6.45 us -> 23.7 us
  waiting for transfers between devices: 36.5 us -> 21.8 us
  starting transfers between devices: 19.7 us -> 15.6 us
    all_to_all x0 -> x1, blocking collectives: none -> 17.5 us  [local(): lax.all_to_all(left, 'row', split_axis=0, concat_axis=1, tiled=True)]
    all_to_all x2 -> x1, waiting for transfers between devices: 25.2 us -> 10.4 us  [local(): lax.all_to_all(jnp.stack(jnp.split(right, lax.axis_size('row'), axis=0)),...]
    another operation x0 -> x18, local copies, waits for them, and re-layouts: none -> 10.9 us  [local(): jnp.stack(jnp.split(right, lax.axis_size('row'), axis=0))]
    unnamed x16 -> x31, local copies, waits for them, and re-layouts: 1.08 us -> 10.2 us
    all_to_all x2 -> x1, starting transfers between devices: 11.7 us -> 7.59 us  [local(): lax.all_to_all(jnp.stack(jnp.split(right, lax.axis_size('row'), axis=0)),...]
    convert_element_type x1 -> x0, local copies, waits for them, and re-layouts: 1.19 us -> none  [local(): (jax.nn.sigmoid(project(w_right_gate)) * project(w_right) * pair_mask[Non...]
  transfers between devices with their start and end apart: 4 -> 3, of which waited for: 3 -> 2; matrix products, arithmetic and copies ran while one was open for 5% -> 3% of each run, Pallas kernels for 0% -> 0%
where the time goes in v1:
time: 102 us; the launch traced here: 101 us
  blocking collectives  32.5 us (32%)
  local copies, waits for them, and re-layouts  23.7 us (23%)
  waiting for transfers between devices  21.8 us (21%)
  starting transfers between devices  15.6 us (15%)
  matrix products  4.94 us (5%)
  other arithmetic  1.95 us (2%)
    all_to_all x1, blocking collectives, local(): lax.all_to_all(left, 'row', split_axis=0, concat_axis=1, tiled=True)  17.5 us
    all_gather x1, blocking collectives, local(): lax.all_gather(left_rows, 'col', axis=2, tiled=True)  15 us
    all_to_all x1, waiting for transfers between devices, local(): lax.all_to_all(triangle, 'row', split_axis=2, concat_axis=1, tiled=True)  11.4 us
    another operation x18, local copies, waits for them, and re-layouts, local(): jnp.stack(jnp.split(right, lax.axis_size('row'), axis=0))  10.9 us
    all_to_all x1, waiting for transfers between devices, local(): lax.all_to_all(jnp.stack(jnp.split(right, lax.axis_size('row'), axis=0)),...  10.4 us
    unnamed x31, local copies, waits for them, and re-layouts  10.2 us
    all_to_all x1, starting transfers between devices, local(): lax.all_to_all(jnp.stack(jnp.split(right, lax.axis_size('row'), axis=0)),...  7.59 us
    all_to_all x1, starting transfers between devices, local(): lax.all_to_all(triangle, 'row', split_axis=2, concat_axis=1, tiled=True)  4.55 us
  transfers between devices with their start and end apart: 3, of which 2 were waited for; matrix products, arithmetic and copies ran while one was open for 3% of the time, Pallas kernels for 0%

profile of v1, /device:TPU:0, one launch (start us, length us, event | category | flops | bytes accessed | tf_op | source)
XLA Modules:
  0.0 100.8 jit_solution(6195479273498588201)
XLA Ops:
  0.0 1.2 %convert_reduce_fusion = f32[12,96]{1,0:T(8,128)S(1)} fusion(bf16[12,96,128]{2,1,0:T(8,128)(2,1)} %param.8), kind=kLoop, calls=%fused_computation.34 | loop fusion | flops 293760 | bytes 299520 | tf_op jit(solution)/shard_map/reduce_sum | solution.py:10
  1.2 0.5 fusion.26
  1.8 0.8 fusion.8
  2.6 0.3 fusion.18
  2.9 0.5 copy-done.2
  3.3 0.5 fusion.17
  3.9 2.4 %slice_bitcast_fusion = (bf16[1,8,12,96]{1,3,2,0:T(8,128)(2,1)S(1)}, bf16[1,8,12,96]{1,3,2,0:T(8,128)(2,1)S(1)}, bf16[1,8,12,96]{1,3,2,0:T(8,128)(2,1)S(1)}, bf1...) fusion(bf16[128,12,96]{0,2,1:T(8,128)(2,1)S(1)} %fusion.17), kind=kLoop, calls=%fused_computation.43 | loop fusion | bytes 589824 | tf_op jit(solution)/shard_map/stack | solution.py:44
  6.3 1.1 %copy.20 = bf16[1,8,12,96]{3,1,2,0:T(8,128)(2,1)S(1)} copy(bf16[1,8,12,96]{1,3,2,0:T(8,128)(2,1)} %get-tuple-element.20) | data formatting | bytes 36864 | tf_op jit(solution)/shard_map/stack | solution.py:44
  7.3 0.6 constant_dynamic-update-slice_fusion.15
  8.0 1.1 %copy.21 = bf16[1,8,12,96]{3,1,2,0:T(8,128)(2,1)S(1)} copy(bf16[1,8,12,96]{1,3,2,0:T(8,128)(2,1)} %get-tuple-element.19) | data formatting | bytes 36864 | tf_op jit(solution)/shard_map/stack | solution.py:44
  9.0 1.1 %copy.22 = bf16[1,8,12,96]{3,1,2,0:T(8,128)(2,1)S(1)} copy(bf16[1,8,12,96]{1,3,2,0:T(8,128)(2,1)} %get-tuple-element.18) | data formatting | bytes 36864 | tf_op jit(solution)/shard_map/stack | solution.py:44
  10.1 1.1 %copy.23 = bf16[1,8,12,96]{3,1,2,0:T(8,128)(2,1)S(1)} copy(bf16[1,8,12,96]{1,3,2,0:T(8,128)(2,1)} %get-tuple-element.17) | data formatting | bytes 36864 | tf_op jit(solution)/shard_map/stack | solution.py:44
  11.2 1.1 %copy.24 = bf16[1,8,12,96]{3,1,2,0:T(8,128)(2,1)S(1)} copy(bf16[1,8,12,96]{1,3,2,0:T(8,128)(2,1)} %get-tuple-element.16) | data formatting | bytes 36864 | tf_op jit(solution)/shard_map/stack | solution.py:44
  12.3 1.1 %copy.25 = bf16[1,8,12,96]{3,1,2,0:T(8,128)(2,1)S(1)} copy(bf16[1,8,12,96]{1,3,2,0:T(8,128)(2,1)} %get-tuple-element.15) | data formatting | bytes 36864 | tf_op jit(solution)/shard_map/stack | solution.py:44
  14.8 0.6 constant_dynamic-update-slice_fusion.14
  15.4 0.6 constant_dynamic-update-slice_fusion.13
  16.0 0.6 constant_dynamic-update-slice_fusion.12
  16.6 0.6 constant_dynamic-update-slice_fusion.11
  17.2 0.6 constant_dynamic-update-slice_fusion.10
  17.8 0.6 constant_dynamic-update-slice_fusion.9
  18.4 0.6 constant_dynamic-update-slice_fusion.8
  19.0 0.6 constant_dynamic-update-slice_fusion.7
  19.6 0.6 constant_dynamic-update-slice_fusion.6
  20.3 0.6 constant_dynamic-update-slice_fusion.5
  20.9 0.6 constant_dynamic-update-slice_fusion.4
  21.5 0.6 constant_dynamic-update-slice_fusion.3
  22.1 0.6 constant_dynamic-update-slice_fusion.2
  22.7 0.6 constant_dynamic-update-slice_fusion.1
  23.3 0.6 constant_dynamic-update-slice_fusion
  23.9 7.6 %all-to-all-start = ((bf16[16,8,12,96]{3,1,2,0:T(8,128)(2,1)}), bf16[16,8,12,96]{3,1,2,0:T(8,128)(2,1)}, u32[]{:S(2)}, u32[]{:S(2)}) async-start(bf16[16,8,12,96]{3,1,2,0:T(8,128)(2,1)} %constant_dynamic-update-slice_fusion), calls=%async_computation | async-start | bytes 786432 | tf_op jit(solution)/shard_map/all_to_all | solution.py:44
  31.5 0.8 fusion.5
  32.3 0.5 fusion.16
  32.8 0.4 copy.37
  33.3 10.4 %all-to-all-done = bf16[16,8,12,96]{3,1,2,0:T(8,128)(2,1)} async-done(((bf16[16,8,12,96]{3,1,2,0:T(8,128)(2,1)}), bf16[16,8,12,96]{3,1,2,0:T(8,128)(2,1)}, u32[]{:S(2)}, u32[]{:S(2)}) %all-to-all-start) | async-done | bytes 294944 | tf_op jit(solution)/shard_map/all_to_all | solution.py:44
  43.7 17.5 %all_to_all.50 = bf16[128,12,96]{2,1,0:T(8,128)(2,1)S(1)} all-to-all(bf16[128,12,96]{2,1,0:T(8,128)(2,1)S(1)} %copy.37), channel_id=1, replica_groups=mesh['row'=16,'col'=2] {'row'}, dimensions={0} | all-to-all | bytes 589824 | tf_op jit(solution)/shard_map/all_to_all | solution.py:42
  61.2 3.5 %all-to-all-start.1 = ((bf16[8,192,96]{2,0,1:T(8,128)(2,1)}), bf16[8,192,96]{2,0,1:T(8,128)(2,1)S(1)}, u32[]{:S(2)}, u32[]{:S(2)}) async-start(bf16[8,192,96]{2,0,1:T(8,128)(2,1)} %bitcast.21), calls=%async_computation.1 | async-start | bytes 786432 | tf_op jit(solution)/shard_map/all_to_all | solution.py:48
  64.8 0.4 copy.40
  65.2 15.0 %all_gather.3 = bf16[8,192,192]{1,0,2:T(8,128)(2,1)S(1)} all-gather(bf16[8,192,96]{1,0,2:T(8,128)(2,1)S(1)} %copy.40), channel_id=1, replica_groups=mesh['row'=16,'col'=2] {'col'}, dimensions={2}, use_global_device_ids=true | all-gather | bytes 884736 | tf_op jit(solution)/shard_map/all_gather | solution.py:51
  80.3 0.4 copy.52
  80.7 0.2 all_to_all.40
  80.9 0.3 fusion.15
  81.2 1.0 copy.42
  82.2 4.5 %all-to-all-start.3 = ((bf16[96,8,192]{0,1,2:T(8,128)(2,1)}), bf16[96,8,192]{0,1,2:T(8,128)(2,1)S(1)}, u32[]{:S(2)}, u32[]{:S(2)}) async-start(bf16[96,8,192]{0,1,2:T(8,128)(2,1)} %copy.42), calls=%async_computation.3 | async-start | bytes 786432 | tf_op jit(solution)/shard_map/all_to_all | solution.py:56
  86.7 0.8 fusion.11
  87.5 11.4 %all-to-all-done.3 = bf16[96,8,192]{0,1,2:T(8,128)(2,1)S(1)} async-done(((bf16[96,8,192]{0,1,2:T(8,128)(2,1)}), bf16[96,8,192]{0,1,2:T(8,128)(2,1)S(1)}, u32[]{:S(2)}, u32[]{:S(2)}) %all-to-all-start.3) | async-done | bytes 294944 | tf_op jit(solution)/shard_map/all_to_all | solution.py:56
  99.0 0.1 multiply_reduce_fusion
  99.2 0.6 copy-done.4
  99.8 1.0 fusion.14
  (33 shorter events, 1.7 us)
Async XLA Ops:
  0.0 1.8 %copy-start = (bf16[128,128]{1,0:T(8,128)(2,1)S(1)}, bf16[128,128]{1,0:T(8,128)(2,1)}, u32[]{:S(2)}) copy-start(bf16[128,128]{1,0:T(8,128)(2,1)} %param.12) | copy-start | bytes 98308
  0.0 1.2 %copy-start.1 = (bf16[12,96,128]{2,1,0:T(8,128)(2,1)S(1)}, bf16[12,96,128]{2,1,0:T(8,128)(2,1)}, u32[]{:S(2)}) copy-start(bf16[12,96,128]{2,1,0:T(8,128)(2,1)} %param.8) | copy-start | bytes 884740
  1.8 0.8 copy-start.7
  2.6 0.8 copy-start.2
  23.9 7.6 %copy-start.5 = (bf16[128,128]{1,0:T(8,128)(2,1)S(1)}, bf16[128,128]{1,0:T(8,128)(2,1)}, u32[]{:S(2)}) copy-start(bf16[128,128]{1,0:T(8,128)(2,1)} %param.10) | copy-start | bytes 98308
  23.9 19.8 %all-to-all-start = ((bf16[16,8,12,96]{3,1,2,0:T(8,128)(2,1)}), bf16[16,8,12,96]{3,1,2,0:T(8,128)(2,1)}, u32[]{:S(2)}, u32[]{:S(2)}) async-start(bf16[16,8,12,96]{3,1,2,0:T(8,128)(2,1)} %constant_dynamic-update-slice_fusion), calls=%async_computation | async-start | bytes 786432 | tf_op jit(solution)/shard_map/all_to_all | solution.py:44
  31.5 0.8 copy-start.3
  61.2 19.0 %all-to-all-start.1 = ((bf16[8,192,96]{2,0,1:T(8,128)(2,1)}), bf16[8,192,96]{2,0,1:T(8,128)(2,1)S(1)}, u32[]{:S(2)}, u32[]{:S(2)}) async-start(bf16[8,192,96]{2,0,1:T(8,128)(2,1)} %bitcast.21), calls=%async_computation.1 | async-start | bytes 786432 | tf_op jit(solution)/shard_map/all_to_all | solution.py:48
  82.2 4.6 %copy-start.6 = (bf16[128,128]{1,0:T(8,128)(2,1)S(1)}, bf16[128,128]{1,0:T(8,128)(2,1)}, u32[]{:S(2)}) copy-start(bf16[128,128]{1,0:T(8,128)(2,1)} %param.14) | copy-start | bytes 98308
  82.2 16.7 %all-to-all-start.3 = ((bf16[96,8,192]{0,1,2:T(8,128)(2,1)}), bf16[96,8,192]{0,1,2:T(8,128)(2,1)S(1)}, u32[]{:S(2)}, u32[]{:S(2)}) async-start(bf16[96,8,192]{0,1,2:T(8,128)(2,1)} %copy.42), calls=%async_computation.3 | async-start | bytes 786432 | tf_op jit(solution)/shard_map/all_to_all | solution.py:56
  99.0 0.8 copy-start.4
